TPU v7x, 512 devices: a 4x2x32 block of a 4x8x32 slice. The times are simulated.
512 devices in a mesh: group: 2 (over y), seq: 128 (over x, z), head: 2 (over core).
Axes of the slice: x: 4, y: 2, z: 32, core: 2. Of those that a mesh axis runs over, the one named last changes fastest.
The devices are a block of a 4x8x32 slice.
Arguments:
- queries: bfloat16 [32768, 3, 2560], P(('group', 'seq'), None, 'head'), parts along dimension 0, may hold values from -6 to 6, as said below
- keys: bfloat16 [32768, 512], P(('group', 'seq'), 'head'), parts along dimension 0, may hold values from -6 to 6, as said below
- values: bfloat16 [32768, 512], P(('group', 'seq'), 'head'), parts along dimension 0, may hold values from -6 to 6
- lengths: int32 [128], P('group'), parts along dimension 0, may hold values from 1 to 1024, 16384 in all
- page_owner: int32 [8192, 4], P(('group', 'seq'), 'head'), parts along dimension 0, may hold values from 0 to 127, as said below
- page_slot: int32 [8192, 4], P(('group', 'seq'), 'head'), parts along dimension 0, may hold values from 0 to 63, as said below
Outputs:
- attended: bfloat16 [32768, 3, 2560], P(('group', 'seq'), None, 'head'), parts along dimension 0
- cache_pages: bfloat16 [32768, 4, 256], P(('group', 'seq', 'head')), parts along dimension 0
There are 2 independent parts, one for each index of `group`. A program takes and returns all parts, laid end to end along the dimension named above; each array names one. Nothing has to cross between parts.
Inputs may be any that keep to these rules, and one draw needn't show every extreme that they name: `page_owner`: for each index g of the head axis, the pages of KV heads g * 2 to g * 2 + 1 held by one index of seq include at most one page for any one owner, and that bound is reached; every owner receives exactly 64 such pages. `page_slot`: the pages that one owner receives for one index of the head axis have distinct slots. `queries`: entries lie within the range; they are of order one. `keys`: entries lie within the range; they are of order one. `lengths`: sum to 16384; the largest is exactly 1024.
All inputs are finite; a program needn't handle non-finite values.
Results may differ from a plain program's by a relative error of at most 0.0029.
Values may be sent and summed in bfloat16 or wider, within the bound.
No kernel may reach another device: no remote copies, remote signals or barrier semaphores. Data moves between devices by JAX's collectives and lax.ppermute only.
A program may use at most 64 MiB of HBM per device.

v0:
```python
import math

import jax
import jax.numpy as jnp
from jax import lax
from jax.sharding import PartitionSpec as P

LAYERS = 3
QPER = 5
HD = 128
PAGE = 4


negative_fill = -1e30


def shifted(x, axis, by):
    count = lax.axis_size(axis)
    pairs = [(i, i + by) for i in range(count) if 0 <= i + by < count]
    return lax.ppermute(x, axis, pairs)


def request_ids(positions, starts):
    return jnp.sum((starts[None, :] <= positions[:, None]).astype(jnp.int32), axis=1) - 1


def shards(queries, keys, values, lengths, page_owner, page_slot):
    tok_rows = keys.shape[0]
    kv_local = keys.shape[1] // HD
    seq_count = lax.axis_size("seq")
    reach = min(8, seq_count // 2)
    mine = lax.axis_index("seq")
    starts = jnp.cumsum(lengths) - lengths
    local_iota = jnp.arange(tok_rows, dtype=jnp.int32)
    query_pos = mine * tok_rows + local_iota
    query_req = request_ids(query_pos, starts)
    grouped = queries.reshape(tok_rows, LAYERS, kv_local, QPER, HD)
    scale = 1.0 / math.sqrt(HD)

    def attend(carry, block, anchor):
        key_pos = anchor * tok_rows + local_iota
        key_req = request_ids(key_pos, starts)
        allowed = (
            (query_req[:, None] == key_req[None, :])
            & (key_pos[None, :] <= query_pos[:, None])
            & (key_pos[None, :] >= 0)
        )
        maxima, totals, summed = carry
        block_keys = block[0].reshape(tok_rows, kv_local, HD)
        block_vals = block[1].reshape(tok_rows, kv_local, HD)
        scores = (
            jnp.einsum("tlcqd,kcd->tlcqk", grouped, block_keys, preferred_element_type=jnp.float32)
            * scale
        )
        wide = allowed[:, None, None, None, :]
        masked = jnp.where(wide, scores, negative_fill)
        fresh = jnp.maximum(maxima, jnp.max(masked, axis=-1))
        shrink = jnp.exp(maxima - fresh)
        weights = jnp.where(wide, jnp.exp(masked - fresh[..., None]), 0.0)
        totals = totals * shrink + jnp.sum(weights, axis=-1)
        product = jnp.einsum(
            "tlcqk,kcd->tlcqd",
            weights.astype(jnp.bfloat16),
            block_vals,
            preferred_element_type=jnp.float32,
        )
        summed = summed * shrink[..., None] + product
        return (fresh, totals, summed)

    stat_shape = (tok_rows, LAYERS, kv_local, QPER)
    carry = (
        jnp.full(stat_shape, negative_fill, jnp.float32),
        jnp.zeros(stat_shape, jnp.float32),
        jnp.zeros(stat_shape + (HD,), jnp.float32),
    )
    pair = jnp.stack([keys, values])
    carry = attend(carry, pair, mine)
    moving = pair
    for step in range(1, reach + 1):
        moving = shifted(moving, "seq", 1)
        carry = attend(carry, moving, mine - step)
    maxima, totals, summed = carry
    attended = (
        (summed / totals[..., None])
        .astype(jnp.bfloat16)
        .reshape(tok_rows, LAYERS, kv_local * QPER * HD)
    )
    pages_dev = tok_rows // PAGE
    slots = pages_dev * kv_local
    capacity = max(1, slots // seq_count)
    key_pages = keys.reshape(pages_dev, PAGE, kv_local, HD)
    val_pages = values.reshape(pages_dev, PAGE, kv_local, HD)
    flat_pages = (
        jnp.concatenate([key_pages, val_pages], axis=3)
        .transpose(0, 2, 1, 3)
        .reshape(slots, PAGE * 2 * HD)
    )
    owner = page_owner.reshape(slots)
    slot = page_slot.reshape(slots)
    number = jnp.arange(slots, dtype=jnp.int32)
    earlier = (owner[None, :] == owner[:, None]) & (number[None, :] < number[:, None])
    rank = jnp.sum(earlier.astype(jnp.int32), axis=1)
    target = owner * capacity + rank
    lanes = jnp.arange(seq_count * capacity, dtype=jnp.int32)
    picker = (lanes[:, None] == target[None, :]).astype(jnp.bfloat16)
    outgoing = jnp.dot(picker, flat_pages, preferred_element_type=jnp.float32).astype(jnp.bfloat16)
    outgoing = outgoing.reshape(seq_count, capacity, PAGE * 2 * HD)
    tags = jnp.dot(
        picker, (slot + 1).astype(jnp.bfloat16), preferred_element_type=jnp.float32
    ).astype(jnp.bfloat16)
    tags = tags.reshape(seq_count, capacity)
    received, got_tags = (
        lax.all_to_all(outgoing, "seq", split_axis=0, concat_axis=0, tiled=True),
        lax.all_to_all(tags, "seq", split_axis=0, concat_axis=0, tiled=True),
    )
    received = received.reshape(seq_count * capacity, PAGE * 2 * HD)
    got_tags = got_tags.reshape(seq_count * capacity).astype(jnp.float32)
    placer = (got_tags[None, :] == (number + 1).astype(jnp.float32)[:, None]).astype(jnp.bfloat16)
    cache_pages = jnp.dot(placer, received, preferred_element_type=jnp.float32).astype(jnp.bfloat16)
    cache_pages = cache_pages.reshape(slots, PAGE, 2 * HD)
    return (attended, cache_pages)


def solution(mesh):
    placed = (
        P(("group", "seq"), None, "head"),
        P(("group", "seq"), "head"),
        P(("group", "seq"), "head"),
        P("group"),
        P(("group", "seq"), "head"),
        P(("group", "seq"), "head"),
    )
    return jax.shard_map(
        shards,
        mesh=mesh,
        in_specs=placed,
        out_specs=(P(("group", "seq"), None, "head"), P(("group", "seq", "head"), None, None)),
        check_vma=False,
    )
```

profile of v0, /device:TPU:38, one launch (start us, length us, event | category | flops | bytes accessed | tf_op | source)
XLA Modules:
  0.0 194.5 jit_solution(1295852395093464614)
XLA Ops:
  0.6 0.8 add_convert_fusion
  1.6 0.8 copy.190
  2.8 0.8 copy.192
  3.6 52.3 %all-to-all-start = ((bf16[128,1,1]{2,1,0:T(2,128)(2,1)}), bf16[128,1,1]{2,1,0:T(2,128)(2,1)}, u32[]{:S(2)}, u32[]{:S(2)}) async-start(bf16[128,1,1]{2,1,0:T(2,128)(2,1)} %copy.192), calls=%async_computation | async-start | bytes 131072 | tf_op jit(solution)/shard_map/all_to_all | solution.py:114
  55.9 1.0 copy.236
  56.8 1.0 copy.163
  57.8 0.7 pad_maximum_fusion
  58.5 3.4 %collective-permute-start = (bf16[2,128,256]{1,2,0:T(8,128)(2,1)}, bf16[2,128,256]{1,2,0:T(8,128)(2,1)}, u32[]{:S(2)}, u32[]{:S(2)}) collective-permute-start(bf16[2,128,256]{1,2,0:T(8,128)(2,1)} %pad_maximum_fusion), channel_id=1, source_target_pairs={{0,2},{2,4},{4,6},{6,8},{8,10},{10,12},{12,14},{14,16},{16,18},{18... | collective-permute-start | bytes 393224 | tf_op jit(solution)/shard_map/ppermute | solution.py:20
  62.1 0.9 reshape.1025
  63.0 0.9 reshape_squeeze_stack.6
  63.8 0.9 reshape.1024
  64.7 0.7 copy.157
  65.6 0.7 sub.217
  66.8 0.7 copy.158
  67.5 1.1 and_and_fusion.8
  68.7 1.0 fusion.10
  69.7 0.8 and_and_fusion.7
  70.5 0.6 add_convert_fusion.1
  71.1 0.6 broadcast.736
  71.7 0.8 reduce.3
  72.6 0.9 reshape.1054
  73.4 5.3 %all-to-all-done = bf16[128,1,1]{2,1,0:T(2,128)(2,1)} async-done(((bf16[128,1,1]{2,1,0:T(2,128)(2,1)}), bf16[128,1,1]{2,1,0:T(2,128)(2,1)}, u32[]{:S(2)}, u32[]{:S(2)}) %all-to-all-start) | async-done | bytes 288 | tf_op jit(solution)/shard_map/all_to_all | solution.py:114
  78.7 22.7 %all-to-all-start.1 = ((bf16[128,2,512]{2,1,0:T(2,128)(2,1)}), bf16[128,2,512]{2,1,0:T(2,128)(2,1)S(1)}, u32[]{:S(2)}, u32[]{:S(2)}) async-start(bf16[128,2,512]{2,1,0:T(2,128)(2,1)} %reshape.1054), calls=%async_computation.1 | async-start | bytes 524288 | tf_op jit(solution)/shard_map/all_to_all | solution.py:113
  101.4 1.9 convert_reduce_fusion
  103.3 0.9 fusion.160
  104.2 3.4 %collective-permute-start.1 = (bf16[2,128,256]{1,2,0:T(8,128)(2,1)}, bf16[2,128,256]{1,2,0:T(8,128)(2,1)S(1)}, u32[]{:S(2)}, u32[]{:S(2)}) collective-permute-start(bf16[2,128,256]{1,2,0:T(8,128)(2,1)} %collective-permute-done), channel_id=1, source_target_pairs={{0,2},{2,4},{4,6},{6,8},{8,10},{10,12},{12,14},{14,16},{16,18},{18... | collective-permute-start | bytes 393224 | tf_op jit(solution)/shard_map/ppermute | solution.py:20
  107.6 1.2 fusion.11
  108.8 16.5 %collective-permute-done.1 = bf16[2,128,256]{1,2,0:T(8,128)(2,1)S(1)} collective-permute-done((bf16[2,128,256]{1,2,0:T(8,128)(2,1)}, bf16[2,128,256]{1,2,0:T(8,128)(2,1)S(1)}, u32[]{:S(2)}, u32[]{:S(2)}) %collective-permute-start.1) | collective-permute-done | bytes 131104 | tf_op jit(solution)/shard_map/ppermute | solution.py:20
  125.3 2.0 %collective-permute-start.2 = (bf16[2,128,256]{1,2,0:T(8,128)(2,1)S(1)}, bf16[2,128,256]{1,2,0:T(8,128)(2,1)S(1)}, u32[]{:S(2)}, u32[]{:S(2)}) collective-permute-start(bf16[2,128,256]{1,2,0:T(8,128)(2,1)S(1)} %collective-permute-done.1), channel_id=1, source_target_pairs={{0,2},{2,4},{4,6},{6,8},{8,10},{10,12},{12,14},{14,16},{16,18},{18... | collective-permute-start | bytes 393224 | tf_op jit(solution)/shard_map/ppermute | solution.py:20
  127.3 0.5 fusion.12
  127.8 6.6 %collective-permute-done.2 = bf16[2,128,256]{1,2,0:T(8,128)(2,1)S(1)} collective-permute-done((bf16[2,128,256]{1,2,0:T(8,128)(2,1)S(1)}, bf16[2,128,256]{1,2,0:T(8,128)(2,1)S(1)}, u32[]{:S(2)}, u32[]{:S(2)}) %collective-permute-start.2) | collective-permute-done | bytes 131104 | tf_op jit(solution)/shard_map/ppermute | solution.py:20
  134.4 2.1 %collective-permute-start.3 = (bf16[2,128,256]{1,2,0:T(8,128)(2,1)S(1)}, bf16[2,128,256]{1,2,0:T(8,128)(2,1)S(1)}, u32[]{:S(2)}, u32[]{:S(2)}) collective-permute-start(bf16[2,128,256]{1,2,0:T(8,128)(2,1)S(1)} %collective-permute-done.2), channel_id=1, source_target_pairs={{0,2},{2,4},{4,6},{6,8},{8,10},{10,12},{12,14},{14,16},{16,18},{18... | collective-permute-start | bytes 393224 | tf_op jit(solution)/shard_map/ppermute | solution.py:20
  136.6 0.5 fusion.13
  137.1 6.3 %collective-permute-done.3 = bf16[2,128,256]{1,2,0:T(8,128)(2,1)S(1)} collective-permute-done((bf16[2,128,256]{1,2,0:T(8,128)(2,1)S(1)}, bf16[2,128,256]{1,2,0:T(8,128)(2,1)S(1)}, u32[]{:S(2)}, u32[]{:S(2)}) %collective-permute-start.3) | collective-permute-done | bytes 131104 | tf_op jit(solution)/shard_map/ppermute | solution.py:20
  143.4 2.0 %collective-permute-start.4 = (bf16[2,128,256]{1,2,0:T(8,128)(2,1)S(1)}, bf16[2,128,256]{1,2,0:T(8,128)(2,1)S(1)}, u32[]{:S(2)}, u32[]{:S(2)}) collective-permute-start(bf16[2,128,256]{1,2,0:T(8,128)(2,1)S(1)} %collective-permute-done.3), channel_id=1, source_target_pairs={{0,2},{2,4},{4,6},{6,8},{8,10},{10,12},{12,14},{14,16},{16,18},{18... | collective-permute-start | bytes 393224 | tf_op jit(solution)/shard_map/ppermute | solution.py:20
  145.9 6.5 %collective-permute-done.4 = bf16[2,128,256]{1,2,0:T(8,128)(2,1)S(1)} collective-permute-done((bf16[2,128,256]{1,2,0:T(8,128)(2,1)S(1)}, bf16[2,128,256]{1,2,0:T(8,128)(2,1)S(1)}, u32[]{:S(2)}, u32[]{:S(2)}) %collective-permute-start.4) | collective-permute-done | bytes 131104 | tf_op jit(solution)/shard_map/ppermute | solution.py:20
  152.4 2.0 %collective-permute-start.5 = (bf16[2,128,256]{1,2,0:T(8,128)(2,1)S(1)}, bf16[2,128,256]{1,2,0:T(8,128)(2,1)S(1)}, u32[]{:S(2)}, u32[]{:S(2)}) collective-permute-start(bf16[2,128,256]{1,2,0:T(8,128)(2,1)S(1)} %collective-permute-done.4), channel_id=1, source_target_pairs={{0,2},{2,4},{4,6},{6,8},{8,10},{10,12},{12,14},{14,16},{16,18},{18... | collective-permute-start | bytes 393224 | tf_op jit(solution)/shard_map/ppermute | solution.py:20
  154.4 0.5 fusion.15
  154.9 6.5 %collective-permute-done.5 = bf16[2,128,256]{1,2,0:T(8,128)(2,1)S(1)} collective-permute-done((bf16[2,128,256]{1,2,0:T(8,128)(2,1)S(1)}, bf16[2,128,256]{1,2,0:T(8,128)(2,1)S(1)}, u32[]{:S(2)}, u32[]{:S(2)}) %collective-permute-start.5) | collective-permute-done | bytes 131104 | tf_op jit(solution)/shard_map/ppermute | solution.py:20
  161.5 2.0 %collective-permute-start.6 = (bf16[2,128,256]{1,2,0:T(8,128)(2,1)S(1)}, bf16[2,128,256]{1,2,0:T(8,128)(2,1)S(1)}, u32[]{:S(2)}, u32[]{:S(2)}) collective-permute-start(bf16[2,128,256]{1,2,0:T(8,128)(2,1)S(1)} %collective-permute-done.5), channel_id=1, source_target_pairs={{0,2},{2,4},{4,6},{6,8},{8,10},{10,12},{12,14},{14,16},{16,18},{18... | collective-permute-start | bytes 393224 | tf_op jit(solution)/shard_map/ppermute | solution.py:20
  163.9 6.9 %collective-permute-done.6 = bf16[2,128,256]{1,2,0:T(8,128)(2,1)S(1)} collective-permute-done((bf16[2,128,256]{1,2,0:T(8,128)(2,1)S(1)}, bf16[2,128,256]{1,2,0:T(8,128)(2,1)S(1)}, u32[]{:S(2)}, u32[]{:S(2)}) %collective-permute-start.6) | collective-permute-done | bytes 131104 | tf_op jit(solution)/shard_map/ppermute | solution.py:20
  170.8 2.0 %collective-permute-start.7 = (bf16[2,128,256]{1,2,0:T(8,128)(2,1)S(1)}, bf16[2,128,256]{1,2,0:T(8,128)(2,1)S(1)}, u32[]{:S(2)}, u32[]{:S(2)}) collective-permute-start(bf16[2,128,256]{1,2,0:T(8,128)(2,1)S(1)} %collective-permute-done.6), channel_id=1, source_target_pairs={{0,2},{2,4},{4,6},{6,8},{8,10},{10,12},{12,14},{14,16},{16,18},{18... | collective-permute-start | bytes 393224 | tf_op jit(solution)/shard_map/ppermute | solution.py:20
  172.7 0.5 fusion.17
  173.3 6.5 %collective-permute-done.7 = bf16[2,128,256]{1,2,0:T(8,128)(2,1)S(1)} collective-permute-done((bf16[2,128,256]{1,2,0:T(8,128)(2,1)S(1)}, bf16[2,128,256]{1,2,0:T(8,128)(2,1)S(1)}, u32[]{:S(2)}, u32[]{:S(2)}) %collective-permute-start.7) | collective-permute-done | bytes 131104 | tf_op jit(solution)/shard_map/ppermute | solution.py:20
  180.3 0.5 fusion.19
  180.9 0.6 fusion.55
  181.5 0.5 fusion.33
  182.0 0.6 fusion.41
  182.6 0.5 fusion.31
  183.1 0.6 fusion.43
  183.7 0.5 fusion.29
  184.3 0.6 fusion.45
  184.9 0.5 fusion.27
  185.4 0.6 fusion.47
  186.0 0.5 fusion.35
  186.5 0.5 fusion.25
  187.0 0.5 fusion.23
  187.6 0.5 fusion.21
  188.2 0.6 fusion.49
  188.8 0.6 fusion.51
  189.4 0.6 fusion.53
  190.0 1.9 fusion.1
  192.0 1.3 copy.196
  193.7 0.7 reshape.1029
  (74 shorter events, 3.6 us)
Async XLA Ops:
  0.6 66.2 %copy-start = (bf16[128,3,1280]{2,0,1:T(8,128)(2,1)S(1)}, bf16[128,3,1280]{2,0,1:T(8,128)(2,1)}, u32[]{:S(2)}) copy-start(bf16[128,3,1280]{2,0,1:T(8,128)(2,1)} %param.6) | copy-start | bytes 2949124
  3.6 75.1 %all-to-all-start = ((bf16[128,1,1]{2,1,0:T(2,128)(2,1)}), bf16[128,1,1]{2,1,0:T(2,128)(2,1)}, u32[]{:S(2)}, u32[]{:S(2)}) async-start(bf16[128,1,1]{2,1,0:T(2,128)(2,1)} %copy.192), calls=%async_computation | async-start | bytes 131072 | tf_op jit(solution)/shard_map/all_to_all | solution.py:114
  58.5 44.8 %collective-permute-start = (bf16[2,128,256]{1,2,0:T(8,128)(2,1)}, bf16[2,128,256]{1,2,0:T(8,128)(2,1)}, u32[]{:S(2)}, u32[]{:S(2)}) collective-permute-start(bf16[2,128,256]{1,2,0:T(8,128)(2,1)} %pad_maximum_fusion), channel_id=1, source_target_pairs={{0,2},{2,4},{4,6},{6,8},{8,10},{10,12},{12,14},{14,16},{16,18},{18... | collective-permute-start | bytes 393224 | tf_op jit(solution)/shard_map/ppermute | solution.py:20
  68.7 1.0 copy-start.8
  73.4 53.9 %copy-start.2 = (pred[128,128]{0,1:T(8,128)(4,1)S(1)}, pred[128,128]{0,1:T(8,128)(4,1)}, u32[]{:S(2)}) copy-start(pred[128,128]{0,1:T(8,128)(4,1)} %get-tuple-element.62) | copy-start | bytes 49156
  78.7 114.5 %all-to-all-start.1 = ((bf16[128,2,512]{2,1,0:T(2,128)(2,1)}), bf16[128,2,512]{2,1,0:T(2,128)(2,1)S(1)}, u32[]{:S(2)}, u32[]{:S(2)}) async-start(bf16[128,2,512]{2,1,0:T(2,128)(2,1)} %reshape.1054), calls=%async_computation.1 | async-start | bytes 524288 | tf_op jit(solution)/shard_map/all_to_all | solution.py:113
  104.2 21.1 %collective-permute-start.1 = (bf16[2,128,256]{1,2,0:T(8,128)(2,1)}, bf16[2,128,256]{1,2,0:T(8,128)(2,1)S(1)}, u32[]{:S(2)}, u32[]{:S(2)}) collective-permute-start(bf16[2,128,256]{1,2,0:T(8,128)(2,1)} %collective-permute-done), channel_id=1, source_target_pairs={{0,2},{2,4},{4,6},{6,8},{8,10},{10,12},{12,14},{14,16},{16,18},{18... | collective-permute-start | bytes 393224 | tf_op jit(solution)/shard_map/ppermute | solution.py:20
  108.8 27.7 %copy-start.3 = (pred[128,128]{0,1:T(8,128)(4,1)S(1)}, pred[128,128]{0,1:T(8,128)(4,1)}, u32[]{:S(2)}) copy-start(pred[128,128]{0,1:T(8,128)(4,1)} %get-tuple-element.55) | copy-start | bytes 49156
  125.3 9.1 %collective-permute-start.2 = (bf16[2,128,256]{1,2,0:T(8,128)(2,1)S(1)}, bf16[2,128,256]{1,2,0:T(8,128)(2,1)S(1)}, u32[]{:S(2)}, u32[]{:S(2)}) collective-permute-start(bf16[2,128,256]{1,2,0:T(8,128)(2,1)S(1)} %collective-permute-done.1), channel_id=1, source_target_pairs={{0,2},{2,4},{4,6},{6,8},{8,10},{10,12},{12,14},{14,16},{16,18},{18... | collective-permute-start | bytes 393224 | tf_op jit(solution)/shard_map/ppermute | solution.py:20
  127.8 17.6 %copy-start.4 = (pred[128,128]{0,1:T(8,128)(4,1)S(1)}, pred[128,128]{0,1:T(8,128)(4,1)}, u32[]{:S(2)}) copy-start(pred[128,128]{0,1:T(8,128)(4,1)} %get-tuple-element.56) | copy-start | bytes 49156
  134.4 9.0 %collective-permute-start.3 = (bf16[2,128,256]{1,2,0:T(8,128)(2,1)S(1)}, bf16[2,128,256]{1,2,0:T(8,128)(2,1)S(1)}, u32[]{:S(2)}, u32[]{:S(2)}) collective-permute-start(bf16[2,128,256]{1,2,0:T(8,128)(2,1)S(1)} %collective-permute-done.2), channel_id=1, source_target_pairs={{0,2},{2,4},{4,6},{6,8},{8,10},{10,12},{12,14},{14,16},{16,18},{18... | collective-permute-start | bytes 393224 | tf_op jit(solution)/shard_map/ppermute | solution.py:20
  137.1 17.3 %copy-start.5 = (pred[128,128]{0,1:T(8,128)(4,1)S(1)}, pred[128,128]{0,1:T(8,128)(4,1)}, u32[]{:S(2)}) copy-start(pred[128,128]{0,1:T(8,128)(4,1)} %get-tuple-element.57) | copy-start | bytes 49156
  143.4 9.0 %collective-permute-start.4 = (bf16[2,128,256]{1,2,0:T(8,128)(2,1)S(1)}, bf16[2,128,256]{1,2,0:T(8,128)(2,1)S(1)}, u32[]{:S(2)}, u32[]{:S(2)}) collective-permute-start(bf16[2,128,256]{1,2,0:T(8,128)(2,1)S(1)} %collective-permute-done.3), channel_id=1, source_target_pairs={{0,2},{2,4},{4,6},{6,8},{8,10},{10,12},{12,14},{14,16},{16,18},{18... | collective-permute-start | bytes 393224 | tf_op jit(solution)/shard_map/ppermute | solution.py:20
  145.9 17.5 %copy-start.6 = (pred[128,128]{0,1:T(8,128)(4,1)S(1)}, pred[128,128]{0,1:T(8,128)(4,1)}, u32[]{:S(2)}) copy-start(pred[128,128]{0,1:T(8,128)(4,1)} %get-tuple-element.58) | copy-start | bytes 49156
  152.4 9.0 %collective-permute-start.5 = (bf16[2,128,256]{1,2,0:T(8,128)(2,1)S(1)}, bf16[2,128,256]{1,2,0:T(8,128)(2,1)S(1)}, u32[]{:S(2)}, u32[]{:S(2)}) collective-permute-start(bf16[2,128,256]{1,2,0:T(8,128)(2,1)S(1)} %collective-permute-done.4), channel_id=1, source_target_pairs={{0,2},{2,4},{4,6},{6,8},{8,10},{10,12},{12,14},{14,16},{16,18},{18... | collective-permute-start | bytes 393224 | tf_op jit(solution)/shard_map/ppermute | solution.py:20
  154.9 17.8 %copy-start.7 = (pred[128,128]{0,1:T(8,128)(4,1)S(1)}, pred[128,128]{0,1:T(8,128)(4,1)}, u32[]{:S(2)}) copy-start(pred[128,128]{0,1:T(8,128)(4,1)} %get-tuple-element.59) | copy-start | bytes 49156
  161.5 9.3 %collective-permute-start.6 = (bf16[2,128,256]{1,2,0:T(8,128)(2,1)S(1)}, bf16[2,128,256]{1,2,0:T(8,128)(2,1)S(1)}, u32[]{:S(2)}, u32[]{:S(2)}) collective-permute-start(bf16[2,128,256]{1,2,0:T(8,128)(2,1)S(1)} %collective-permute-done.5), channel_id=1, source_target_pairs={{0,2},{2,4},{4,6},{6,8},{8,10},{10,12},{12,14},{14,16},{16,18},{18... | collective-permute-start | bytes 393224 | tf_op jit(solution)/shard_map/ppermute | solution.py:20
  170.8 9.0 %collective-permute-start.7 = (bf16[2,128,256]{1,2,0:T(8,128)(2,1)S(1)}, bf16[2,128,256]{1,2,0:T(8,128)(2,1)S(1)}, u32[]{:S(2)}, u32[]{:S(2)}) collective-permute-start(bf16[2,128,256]{1,2,0:T(8,128)(2,1)S(1)} %collective-permute-done.6), channel_id=1, source_target_pairs={{0,2},{2,4},{4,6},{6,8},{8,10},{10,12},{12,14},{14,16},{16,18},{18... | collective-permute-start | bytes 393224 | tf_op jit(solution)/shard_map/ppermute | solution.py:20
  173.2 7.0 %copy-start.10 = (f32[128,3,2,5]{0,3,1,2:T(8,128)S(1)}, f32[128,3,2,5]{0,3,1,2:T(8,128)}, u32[]{:S(2)}) copy-start(f32[128,3,2,5]{0,3,1,2:T(8,128)} %get-tuple-element.79) | copy-start | bytes 46084
  173.2 7.1 %copy-start.9 = (pred[128,128]{0,1:T(8,128)(4,1)S(1)}, pred[128,128]{0,1:T(8,128)(4,1)}, u32[]{:S(2)}) copy-start(pred[128,128]{0,1:T(8,128)(4,1)} %copy-done.8) | copy-start | bytes 49156
  186.5 1.1 copy-start.1
  191.9 1.6 copy-start.11
where the time goes:
time: 195 us; the launch traced here: 194 us
  starting transfers between devices  93.7 us (48%)
  waiting for transfers between devices  61.2 us (31%)
  matrix products  12.9 us (7%)
  other arithmetic  12.8 us (7%)
  local copies, waits for them, and re-layouts  12.6 us (6%)
    ppermute x8, waiting for transfers between devices, shifted(): return lax.ppermute(x, axis, pairs)  55.8 us
    all_to_all x1, starting transfers between devices, shards(): lax.all_to_all(tags, 'seq', split_axis=0, concat_axis=0, tiled=True)  52.3 us
    all_to_all x1, starting transfers between devices, shards(): lax.all_to_all(outgoing, 'seq', split_axis=0, concat_axis=0, tiled=True)  22.7 us
    ppermute x8, starting transfers between devices, shifted(): return lax.ppermute(x, axis, pairs)  18.7 us
    dot_general x9, matrix products, attend(): jnp.einsum('tlcqk,kcd->tlcqd', weights.astype(jnp.bfloat16), block_vals,...  6.68 us
    dot_general x9, matrix products, attend(): jnp.einsum('tlcqd,kcd->tlcqk', grouped, block_keys, preferred_element_typ...  5.62 us
    all_to_all x1, waiting for transfers between devices, shards(): lax.all_to_all(tags, 'seq', split_axis=0, concat_axis=0, tiled=True)  5.31 us
    unnamed x31, local copies, waits for them, and re-layouts  4.84 us
  transfers between devices with their start and end apart: 10, of which 8 were waited for; matrix products, arithmetic and copies ran while one was open for 18% of the time, Pallas kernels for 0%

commit v1 on v0

v1 whole, which is shorter than its diff:
```python
import math

import jax
import jax.numpy as jnp
from jax import lax
from jax.experimental import pallas as pl
from jax.experimental.pallas import tpu as pltpu
from jax.sharding import PartitionSpec as P


QPER = 5
HD = 128
PAGE = 4
CHUNKS = PAGE + 1
NEG = -1e30
F32 = jnp.float32
BF16 = jnp.bfloat16

NT = (((1,), (1,)), ((), ()))
NN = (((1,), (0,)), ((), ()))
TN = (((0,), (0,)), ((), ()))


def dot(a, b, dims=NN):
    return lax.dot_general(a, b, dims, preferred_element_type=F32)


def shifted(x, by):
    count = lax.axis_size("seq")
    pairs = [(i, i + by) for i in range(count - by)]
    return lax.ppermute(x, "seq", pairs)


def block_kernel(keys_ref, vals_ref, out_ref):
    for c in range(2):
        out_ref[c] = keys_ref[:, c * HD : (c + 1) * HD]
        out_ref[2 + c] = vals_ref[:, c * HD : (c + 1) * HD].T


def kv_block(keys, values):
    rows = keys.shape[0]
    return pl.pallas_call(
        block_kernel,
        out_shape=jax.ShapeDtypeStruct((4, HD, rows), BF16),
        name="kv_block",
    )(keys, values)


def pack_kernel(keys_ref, vals_ref, owner_ref, slot_ref, out_ref):
    rows = keys_ref.shape[0]
    pages = rows // PAGE
    per = CHUNKS * 2
    total = out_ref.shape[0]
    page_i = lax.broadcasted_iota(jnp.int32, (pages, rows), 0)
    tok_i = lax.broadcasted_iota(jnp.int32, (pages, rows), 1)
    spread = (tok_i // PAGE == page_i).astype(BF16)
    owner = dot(owner_ref[...].astype(BF16), spread).astype(jnp.int32)
    slot = dot(slot_ref[...].astype(BF16), spread).astype(jnp.int32)
    within = lax.broadcasted_iota(jnp.int32, (1, rows), 1) % PAGE
    keyed, tagged, onehot = [], [], []
    lane_id = lax.broadcasted_iota(jnp.int32, (HD, rows), 0)
    for c in range(2):
        base = owner[c : c + 1] * per
        keyed += [base + within * 2, base + within * 2 + 1]
        tagged.append(jnp.where(within == 0, base + PAGE * 2, -1))
        onehot.append((slot[c : c + 1] == lane_id).astype(BF16))
    parts = []
    for c in range(2):
        parts += [keys_ref[:, c * HD : (c + 1) * HD], vals_ref[:, c * HD : (c + 1) * HD]]
    step = 2 * HD
    for begin in range(0, total, step):
        row = begin + lax.broadcasted_iota(jnp.int32, (step, rows), 0)
        acc = jnp.zeros((step, HD), F32)
        for key, part in zip(keyed, parts):
            acc += dot((row == key).astype(BF16), part)
        for key, hot in zip(tagged, onehot):
            acc += dot((row == key).astype(BF16), hot, NT)
        out_ref[begin : begin + step] = acc.astype(BF16)


def pack_pages(keys, values, owner, slot, seq_count):
    return pl.pallas_call(
        pack_kernel,
        out_shape=jax.ShapeDtypeStruct((seq_count * CHUNKS * 2, HD), BF16),
        name="pack_pages",
    )(keys, values, owner, slot)


def place_kernel(got_ref, out_ref):
    total = got_ref.shape[0]
    per = CHUNKS * 2
    sources = total // per
    slots = out_ref.shape[0] // (PAGE * 2)
    got = got_ref[...]
    src = lax.broadcasted_iota(jnp.int32, (sources, total), 0)
    row = lax.broadcasted_iota(jnp.int32, (sources, total), 1)
    pick = (row == src * per + PAGE * 2).astype(BF16)
    hot = dot(pick, got).astype(BF16)[:, :slots]
    owns = (row // per == src).astype(BF16)
    chosen = dot(hot, owns, TN).astype(BF16)
    dst = lax.broadcasted_iota(jnp.int32, (slots * PAGE * 2, slots), 0)
    slot = lax.broadcasted_iota(jnp.int32, (slots * PAGE * 2, slots), 1)
    wide = dot((dst // (PAGE * 2) == slot).astype(BF16), chosen)
    place = lax.broadcasted_iota(jnp.int32, wide.shape, 0) % (PAGE * 2)
    want = (place % PAGE) * 2 + place // PAGE
    have = lax.broadcasted_iota(jnp.int32, wide.shape, 1) % per
    out_ref[...] = dot(jnp.where(want == have, wide, 0.0).astype(BF16), got).astype(BF16)


def place_pages(got, slots):
    return pl.pallas_call(
        place_kernel,
        out_shape=jax.ShapeDtypeStruct((slots * PAGE * 2, HD), BF16),
        name="place_pages",
    )(got)


def attend_kernel(groups, first, final, *refs):
    refs = list(refs)
    mine_ref, lens_ref, q_ref = refs[:3]
    arrays = 1 + max(g[0] for g in groups)
    kv = refs[3 : 3 + arrays]
    rest = refs[3 + arrays :]
    if not first:
        top_in, tot_in, acc_in = rest[:3]
        rest = rest[3:]
    if final:
        out_ref = rest[0]
        top_ref, tot_ref, acc_ref = rest[1:]
    else:
        top_ref, tot_ref, acc_ref = rest
    rows = q_ref.shape[1]
    head = pl.program_id(0)
    reqs = lens_ref.shape[1]
    base = mine_ref[0] * rows
    lens = jnp.broadcast_to(lens_ref[...], (reqs, reqs)).astype(F32)
    r_i = lax.broadcasted_iota(jnp.int32, (reqs, reqs), 0)
    e_i = lax.broadcasted_iota(jnp.int32, (reqs, reqs), 1)
    starts = jnp.sum(jnp.where(e_i < r_i, lens, 0.0), axis=1, keepdims=True) - base.astype(F32)
    lane = lax.broadcasted_iota(jnp.int32, (1, rows), 1)
    known = jnp.where(starts <= lane.astype(F32), starts, -3e7)
    begin = jnp.max(known, axis=0, keepdims=True).astype(jnp.int32)
    earliest = jnp.min(begin)
    key_i = lax.broadcasted_iota(jnp.int32, (rows, rows), 0)
    qry_i = lax.broadcasted_iota(jnp.int32, (rows, rows), 1)
    factor = math.log2(math.e) / math.sqrt(HD)

    if not first:
        top_ref[...] = top_in[...]
        tot_ref[...] = tot_in[...]
        acc_ref[...] = acc_in[...]

    def block(position, source, index, distance):
        ref = kv[source]
        at = (lambda j: ref[j]) if index is None else (lambda j: ref[index, j])
        k_blk = at(head)
        vt_blk = at(2 + head)
        if distance == 0:
            allowed = (key_i >= begin) & (key_i <= qry_i)
        else:
            allowed = key_i >= begin + distance * rows
        for q in range(QPER):
            queries = q_ref[0, :, q * HD : (q + 1) * HD]
            scores = jnp.where(allowed, dot(k_blk, queries, NT) * factor, NEG)
            best = jnp.max(scores, axis=0, keepdims=True)
            if first and position == 0:
                weights = jnp.exp2(scores - best)
                top_ref[0, 0, q : q + 1] = best
                tot_ref[0, 0, q : q + 1] = jnp.sum(weights, axis=0, keepdims=True)
                acc_ref[0, 0, q] = dot(vt_blk, weights.astype(BF16))
            else:
                old = top_ref[0, 0, q : q + 1]
                fresh = jnp.maximum(old, best)
                shrink = jnp.exp2(old - fresh)
                weights = jnp.exp2(scores - fresh)
                top_ref[0, 0, q : q + 1] = fresh
                tot_ref[0, 0, q : q + 1] = tot_ref[0, 0, q : q + 1] * shrink + jnp.sum(
                    weights, axis=0, keepdims=True
                )
                acc_ref[0, 0, q] = acc_ref[0, 0, q] * shrink + dot(vt_blk, weights.astype(BF16))

    for position, (source, index, distance) in enumerate(groups):
        if distance == 0:
            block(position, source, index, distance)
        else:

            @pl.when(earliest < rows - distance * rows)
            def _(position=position, source=source, index=index, distance=distance):
                block(position, source, index, distance)

    if final:
        for q in range(QPER):
            result = acc_ref[0, 0, q] * (1.0 / tot_ref[0, 0, q : q + 1])
            out_ref[0, :, q * HD : (q + 1) * HD] = result.T.astype(BF16)


def attend(mine, lengths, queries, arrays, groups, state, final):
    layers, rows, width = queries.shape
    heads = width // (QPER * HD)
    first = state is None
    grid = (heads, layers)
    stat = pl.BlockSpec((1, 1, 8, rows), lambda c, l: (c, l, 0, 0))
    accs = pl.BlockSpec((1, 1, QPER, HD, rows), lambda c, l: (c, l, 0, 0, 0))
    q_spec = pl.BlockSpec((1, rows, QPER * HD), lambda c, l: (l, 0, c))
    in_specs = [
        pl.BlockSpec(memory_space=pltpu.SMEM),
        pl.BlockSpec(lengths.shape, lambda c, l: (0, 0)),
        q_spec,
    ]
    for a in arrays:
        in_specs.append(pl.BlockSpec(a.shape, lambda c, l, n=a.ndim: (0,) * n))
    state_shapes = [
        jax.ShapeDtypeStruct((heads, layers, 8, rows), F32),
        jax.ShapeDtypeStruct((heads, layers, 8, rows), F32),
        jax.ShapeDtypeStruct((heads, layers, QPER, HD, rows), F32),
    ]
    operands = [mine, lengths, queries, *arrays]
    if not first:
        in_specs += [stat, stat, accs]
        operands += list(state)
    if final:
        out_shape = jax.ShapeDtypeStruct(queries.shape, BF16)
        out_specs = q_spec
        scratch = [
            pltpu.VMEM((1, 1, 8, rows), F32),
            pltpu.VMEM((1, 1, 8, rows), F32),
            pltpu.VMEM((1, 1, QPER, HD, rows), F32),
        ]
    else:
        out_shape, out_specs, scratch = state_shapes, [stat, stat, accs], []

    def kernel(*refs):
        attend_kernel(groups, first, final, *refs)

    return pl.pallas_call(
        kernel,
        grid=grid,
        in_specs=in_specs,
        out_specs=out_specs,
        out_shape=out_shape,
        scratch_shapes=scratch,
        name="attend_last" if final else "attend_part",
    )(*operands)


def shards(queries, keys, values, lengths, page_owner, page_slot):
    tok_rows = keys.shape[0]
    slots = tok_rows // PAGE * 2
    seq_count = lax.axis_size("seq")
    mine = lax.axis_index("seq").astype(jnp.int32).reshape(1)
    lens = lengths.reshape(1, -1)
    flat_q = queries.transpose(1, 0, 2)

    own = kv_block(keys, values)
    b6 = shifted(own, 6)
    b3 = shifted(own, 3)
    b1 = shifted(own, 1)

    outgoing = pack_pages(keys, values, page_owner.T, page_slot.T, seq_count)
    got = lax.all_to_all(
        outgoing.reshape(seq_count, CHUNKS, 2, HD), "seq", split_axis=0, concat_axis=0, tiled=True
    )

    b247 = shifted(jnp.stack([b1, b3, b6]), 1)
    state = attend(
        mine, lens, flat_q, [own, b1, b3, b6],
        [(0, None, 0), (1, None, 1), (2, None, 3), (3, None, 6)], None, False,
    )
    b58 = shifted(b247[1:], 1)
    state = attend(mine, lens, flat_q, [b247], [(0, 0, 2), (0, 1, 4), (0, 2, 7)], state, False)
    out = attend(mine, lens, flat_q, [b58], [(0, 0, 5), (0, 1, 8)], state, True)
    attended = out.transpose(1, 0, 2)

    placed = place_pages(got.reshape(seq_count * CHUNKS * 2, HD), slots)
    cache_pages = (
        placed.reshape(slots, 2, PAGE, HD).transpose(0, 2, 1, 3).reshape(slots, PAGE, 2 * HD)
    )
    return (attended, cache_pages)


def solution(mesh):
    placed = (
        P(("group", "seq"), None, "head"),
        P(("group", "seq"), "head"),
        P(("group", "seq"), "head"),
        P("group"),
        P(("group", "seq"), "head"),
        P(("group", "seq"), "head"),
    )
    return jax.shard_map(
        shards,
        mesh=mesh,
        in_specs=placed,
        out_specs=(P(("group", "seq"), None, "head"), P(("group", "seq", "head"), None, None)),
        check_vma=False,
    )
```

time: 195 us -> 202 us (1.036)
  the two profiles are of different devices: /device:TPU:38 before, /device:TPU:174 now
where the time goes in v1:
time: 202 us; the launch traced here: 201 us
  Pallas kernels  79.4 us (39%)
  starting transfers between devices  76.2 us (38%)
  waiting for transfers between devices  43.3 us (21%)
    pallas_call x3, Pallas kernels, attend(): pl.pallas_call(kernel, grid=grid, in_specs=in_specs, out_specs=out_specs,...  72.4 us
    all_to_all x1, starting transfers between devices, shards(): lax.all_to_all(outgoing.reshape(seq_count, CHUNKS, 2, HD), 'seq', split_a...  49.6 us
    ppermute x5, waiting for transfers between devices, shifted(): return lax.ppermute(x, 'seq', pairs)  43.3 us
    ppermute x5, starting transfers between devices, shifted(): return lax.ppermute(x, 'seq', pairs)  26.6 us
  transfers between devices with their start and end apart: 6, of which 4 were waited for; matrix products, arithmetic and copies ran while one was open for 0% of the time, Pallas kernels for 37%

profile of v1, /device:TPU:174, one launch (start us, length us, event | category | flops | bytes accessed | tf_op | source)
XLA Modules:
  0.0 201.1 jit_solution(9463547524311011392)
XLA Ops:
  0.6 2.4 %pack_pages.1 = bf16[1280,128]{1,0:T(8,128)(2,1)} custom-call(bf16[128,256]{1,0:T(8,128)(2,1)} %keys_ref.3, bf16[128,256]{1,0:T(8,128)(2,1)} %vals_ref.3, s32[2,32]{1,0:T(2,128)} %bitcast.29, s32[2,32]{1,0:T(2,128)} %bitcast.30), custom_call_target="tpu_custom_call" | custom-call | tf_op jit(solution)/shard_map/pack_pages/pallas_call | solution.py:82
  3.0 49.6 %all-to-all-start = ((bf16[128,5,2,128]{3,2,1,0:T(2,128)(2,1)}), bf16[128,5,2,128]{3,2,1,0:T(2,128)(2,1)S(1)}, u32[]{:S(2)}, u32[]{:S(2)}) async-start(bf16[128,5,2,128]{3,2,1,0:T(2,128)(2,1)} %bitcast.20), calls=%async_computation | async-start | bytes 655360 | tf_op jit(solution)/shard_map/all_to_all | solution.py:260
  52.6 1.6 kv_block.1.refs_3_
  54.2 3.4 %collective-permute-start = (bf16[4,128,128]{2,1,0:T(8,128)(2,1)}, bf16[4,128,128]{2,1,0:T(8,128)(2,1)S(1)}, u32[]{:S(2)}, u32[]{:S(2)}) collective-permute-start(bf16[4,128,128]{2,1,0:T(8,128)(2,1)} %kv_block.1.refs_3_), channel_id=1, source_target_pairs={{0,2},{2,4},{4,6},{6,8},{8,10},{10,12},{12,14},{14,16},{16,18},{18... | collective-permute-start | bytes 393224 | tf_op jit(solution)/shard_map/ppermute | solution.py:31
  57.6 6.5 %collective-permute-start.1 = (bf16[4,128,128]{2,1,0:T(8,128)(2,1)}, bf16[4,128,128]{2,1,0:T(8,128)(2,1)S(1)}, u32[]{:S(2)}, u32[]{:S(2)}) collective-permute-start(bf16[4,128,128]{2,1,0:T(8,128)(2,1)} %kv_block.1.refs_3_), channel_id=1, source_target_pairs={{0,6},{2,8},{4,10},{6,12},{8,14},{10,16},{12,18},{14,20},{16,22},{... | collective-permute-start | bytes 393224 | tf_op jit(solution)/shard_map/ppermute | solution.py:31
  64.1 10.4 %collective-permute-start.2 = (bf16[4,128,128]{2,1,0:T(8,128)(2,1)}, bf16[4,128,128]{2,1,0:T(8,128)(2,1)S(1)}, u32[]{:S(2)}, u32[]{:S(2)}) collective-permute-start(bf16[4,128,128]{2,1,0:T(8,128)(2,1)} %kv_block.1.refs_3_), channel_id=1, source_target_pairs={{0,12},{2,14},{4,16},{6,18},{8,20},{10,22},{12,24},{14,26},{16,28}... | collective-permute-start | bytes 393224 | tf_op jit(solution)/shard_map/ppermute | solution.py:31
  74.6 13.1 %collective-permute-done.refs_4_ = bf16[4,128,128]{2,1,0:T(8,128)(2,1)S(1)} collective-permute-done((bf16[4,128,128]{2,1,0:T(8,128)(2,1)}, bf16[4,128,128]{2,1,0:T(8,128)(2,1)S(1)}, u32[]{:S(2)}, u32[]{:S(2)}) %collective-permute-start) | collective-permute-done | bytes 131104 | tf_op jit(solution)/shard_map/ppermute | solution.py:31
  87.7 0.0 copy-start.2
  87.7 7.8 %collective-permute-done.1.refs_5_ = bf16[4,128,128]{2,1,0:T(8,128)(2,1)S(1)} collective-permute-done((bf16[4,128,128]{2,1,0:T(8,128)(2,1)}, bf16[4,128,128]{2,1,0:T(8,128)(2,1)S(1)}, u32[]{:S(2)}, u32[]{:S(2)}) %collective-permute-start.1) | collective-permute-done | bytes 131104 | tf_op jit(solution)/shard_map/ppermute | solution.py:31
  95.5 0.0 copy-start.3
  95.5 15.1 %collective-permute-done.2.refs_6_ = bf16[4,128,128]{2,1,0:T(8,128)(2,1)S(1)} collective-permute-done((bf16[4,128,128]{2,1,0:T(8,128)(2,1)}, bf16[4,128,128]{2,1,0:T(8,128)(2,1)S(1)}, u32[]{:S(2)}, u32[]{:S(2)}) %collective-permute-start.2) | collective-permute-done | bytes 131104 | tf_op jit(solution)/shard_map/ppermute | solution.py:31
  110.7 0.0 copy-start.4
  110.7 3.8 %collective-permute-start.3 = (bf16[3,4,128,128]{3,2,1,0:T(8,128)(2,1)S(1)}, bf16[3,4,128,128]{3,2,1,0:T(8,128)(2,1)S(1)}, u32[]{:S(2)}, u32[]{:S(2)}) collective-permute-start(bf16[3,4,128,128]{3,2,1,0:T(8,128)(2,1)S(1)} %pad_maximum_fusion), channel_id=1, source_target_pairs={{0,2},{2,4},{4,6},{6,8},{8,10},{10,12},{12,14},{14,16},{16,18},{18... | collective-permute-start | bytes 1179656 | tf_op jit(solution)/shard_map/ppermute | solution.py:31
  114.5 7.2 %collective-permute-done.3.refs_3_ = bf16[3,4,128,128]{3,2,1,0:T(8,128)(2,1)S(1)} collective-permute-done((bf16[3,4,128,128]{3,2,1,0:T(8,128)(2,1)S(1)}, bf16[3,4,128,128]{3,2,1,0:T(8,128)(2,1)S(1)}, u32[]{:S(2)}, u32[]{:S(2)}) %collective-permute-start.3) | collective-permute-done | bytes 393248 | tf_op jit(solution)/shard_map/ppermute | solution.py:31
  121.7 0.0 copy-start.1
  121.8 2.5 %collective-permute-start.4 = (bf16[2,4,128,128]{3,2,1,0:T(8,128)(2,1)S(1)}, bf16[2,4,128,128]{3,2,1,0:T(8,128)(2,1)S(1)}, u32[]{:S(2)}, u32[]{:S(2)}) collective-permute-start(bf16[2,4,128,128]{3,2,1,0:T(8,128)(2,1)S(1)} %slice.4), channel_id=1, source_target_pairs={{0,2},{2,4},{4,6},{6,8},{8,10},{10,12},{12,14},{14,16},{16,18},{18... | collective-permute-start | bytes 786440 | tf_op jit(solution)/shard_map/ppermute | solution.py:31
  124.2 0.0 copy-done.2
  124.2 0.0 copy-done.3
  124.3 0.0 copy-done.4
  124.3 28.9 %attend_part.2 = (f32[2,3,8,128]{3,2,1,0:T(8,128)}, f32[2,3,8,128]{3,2,1,0:T(8,128)}, f32[2,3,5,128,128]{4,3,2,1,0:T(8,128)}) custom-call(s32[1]{0:T(128)} %bitcast.refs_0_, s32[1,64]{1,0:T(1,128)} %bitcast.26, bf16[3,128,1280]{2,1,0:T(8,128)(2,1)} %bitcast.16, bf16[4,128,128]{2,1,0:T(8,128)(2,1)} %kv_block.1.refs_3_, bf16[4,128,128]{2,1,0:T(8,128)(2,1)} %copy-done.2, ...), custom_call_target="tpu_custom_call" | custom-call | tf_op jit(solution)/shard_map/attend_part/pallas_call | solution.py:235
  153.2 0.0 copy-done.1
  153.2 24.9 %attend_part.3 = (f32[2,3,8,128]{3,2,1,0:T(8,128)}, f32[2,3,8,128]{3,2,1,0:T(8,128)}, f32[2,3,5,128,128]{4,3,2,1,0:T(8,128)}) custom-call(s32[1]{0:T(128)} %bitcast.refs_0_, s32[1,64]{1,0:T(1,128)} %bitcast.27, bf16[3,128,1280]{2,1,0:T(8,128)(2,1)} %bitcast.17, bf16[3,4,128,128]{3,2,1,0:T(8,128)(2,1)} %copy-done.1, ...), custom_call_target="tpu_custom_call" | custom-call | tf_op jit(solution)/shard_map/attend_part/pallas_call | solution.py:235
  178.1 0.0 collective-permute-done.4.refs_3_
  178.1 0.0 copy-start.5
  178.1 0.7 copy-done.5
  178.8 18.6 %attend_last.1 = bf16[3,128,1280]{2,1,0:T(8,128)(2,1)} custom-call(s32[1]{0:T(128)} %bitcast.refs_0_, s32[1,64]{1,0:T(1,128)} %bitcast.28, bf16[3,128,1280]{2,1,0:T(8,128)(2,1)} %bitcast.18, bf16[2,4,128,128]{3,2,1,0:T(8,128)(2,1)} %copy-done.5, f32[2,3,8,128]{3,2,1,0:T(8,128)} %get-tuple-element.11.refs_4_, f32[2,3,8,128]{3,2,1,0:T(8,128)} %get-tuple-element.12.refs_5_, ...), custom_call_target="tpu_custom_call" | custom-call | tf_op jit(solution)/shard_map/attend_last/pallas_call | solution.py:235
  197.4 0.0 all-to-all-done
  197.4 0.0 copy-start
  197.4 0.7 copy-done
  198.1 3.0 %place_pages.1 = bf16[512,128]{1,0:T(8,128)(2,1)} custom-call(bf16[1280,128]{1,0:T(8,128)(2,1)} %bitcast.19), custom_call_target="tpu_custom_call" | custom-call | tf_op jit(solution)/shard_map/place_pages/pallas_call | solution.py:111
  (2 shorter events, 0.1 us)
Async XLA Ops:
  3.0 194.4 %all-to-all-start = ((bf16[128,5,2,128]{3,2,1,0:T(2,128)(2,1)}), bf16[128,5,2,128]{3,2,1,0:T(2,128)(2,1)S(1)}, u32[]{:S(2)}, u32[]{:S(2)}) async-start(bf16[128,5,2,128]{3,2,1,0:T(2,128)(2,1)} %bitcast.20), calls=%async_computation | async-start | bytes 655360 | tf_op jit(solution)/shard_map/all_to_all | solution.py:260
  54.2 33.5 %collective-permute-start = (bf16[4,128,128]{2,1,0:T(8,128)(2,1)}, bf16[4,128,128]{2,1,0:T(8,128)(2,1)S(1)}, u32[]{:S(2)}, u32[]{:S(2)}) collective-permute-start(bf16[4,128,128]{2,1,0:T(8,128)(2,1)} %kv_block.1.refs_3_), channel_id=1, source_target_pairs={{0,2},{2,4},{4,6},{6,8},{8,10},{10,12},{12,14},{14,16},{16,18},{18... | collective-permute-start | bytes 393224 | tf_op jit(solution)/shard_map/ppermute | solution.py:31
  57.6 37.9 %collective-permute-start.1 = (bf16[4,128,128]{2,1,0:T(8,128)(2,1)}, bf16[4,128,128]{2,1,0:T(8,128)(2,1)S(1)}, u32[]{:S(2)}, u32[]{:S(2)}) collective-permute-start(bf16[4,128,128]{2,1,0:T(8,128)(2,1)} %kv_block.1.refs_3_), channel_id=1, source_target_pairs={{0,6},{2,8},{4,10},{6,12},{8,14},{10,16},{12,18},{14,20},{16,22},{... | collective-permute-start | bytes 393224 | tf_op jit(solution)/shard_map/ppermute | solution.py:31
  64.1 46.5 %collective-permute-start.2 = (bf16[4,128,128]{2,1,0:T(8,128)(2,1)}, bf16[4,128,128]{2,1,0:T(8,128)(2,1)S(1)}, u32[]{:S(2)}, u32[]{:S(2)}) collective-permute-start(bf16[4,128,128]{2,1,0:T(8,128)(2,1)} %kv_block.1.refs_3_), channel_id=1, source_target_pairs={{0,12},{2,14},{4,16},{6,18},{8,20},{10,22},{12,24},{14,26},{16,28}... | collective-permute-start | bytes 393224 | tf_op jit(solution)/shard_map/ppermute | solution.py:31
  87.7 36.6 %copy-start.2 = (bf16[4,128,128]{2,1,0:T(8,128)(2,1)}, bf16[4,128,128]{2,1,0:T(8,128)(2,1)S(1)}, u32[]{:S(2)}) copy-start(bf16[4,128,128]{2,1,0:T(8,128)(2,1)S(1)} %collective-permute-done.refs_4_) | copy-start | bytes 393220
  95.5 28.7 %copy-start.3 = (bf16[4,128,128]{2,1,0:T(8,128)(2,1)}, bf16[4,128,128]{2,1,0:T(8,128)(2,1)S(1)}, u32[]{:S(2)}) copy-start(bf16[4,128,128]{2,1,0:T(8,128)(2,1)S(1)} %collective-permute-done.1.refs_5_) | copy-start | bytes 393220
  110.7 13.6 %copy-start.4 = (bf16[4,128,128]{2,1,0:T(8,128)(2,1)}, bf16[4,128,128]{2,1,0:T(8,128)(2,1)S(1)}, u32[]{:S(2)}) copy-start(bf16[4,128,128]{2,1,0:T(8,128)(2,1)S(1)} %collective-permute-done.2.refs_6_) | copy-start | bytes 393220
  110.7 11.0 %collective-permute-start.3 = (bf16[3,4,128,128]{3,2,1,0:T(8,128)(2,1)S(1)}, bf16[3,4,128,128]{3,2,1,0:T(8,128)(2,1)S(1)}, u32[]{:S(2)}, u32[]{:S(2)}) collective-permute-start(bf16[3,4,128,128]{3,2,1,0:T(8,128)(2,1)S(1)} %pad_maximum_fusion), channel_id=1, source_target_pairs={{0,2},{2,4},{4,6},{6,8},{8,10},{10,12},{12,14},{14,16},{16,18},{18... | collective-permute-start | bytes 1179656 | tf_op jit(solution)/shard_map/ppermute | solution.py:31
  121.7 31.4 %copy-start.1 = (bf16[3,4,128,128]{3,2,1,0:T(8,128)(2,1)}, bf16[3,4,128,128]{3,2,1,0:T(8,128)(2,1)S(1)}, u32[]{:S(2)}) copy-start(bf16[3,4,128,128]{3,2,1,0:T(8,128)(2,1)S(1)} %collective-permute-done.3.refs_3_) | copy-start | bytes 1179652
  121.8 56.3 %collective-permute-start.4 = (bf16[2,4,128,128]{3,2,1,0:T(8,128)(2,1)S(1)}, bf16[2,4,128,128]{3,2,1,0:T(8,128)(2,1)S(1)}, u32[]{:S(2)}, u32[]{:S(2)}) collective-permute-start(bf16[2,4,128,128]{3,2,1,0:T(8,128)(2,1)S(1)} %slice.4), channel_id=1, source_target_pairs={{0,2},{2,4},{4,6},{6,8},{8,10},{10,12},{12,14},{14,16},{16,18},{18... | collective-permute-start | bytes 786440 | tf_op jit(solution)/shard_map/ppermute | solution.py:31
  178.1 0.7 copy-start.5
  197.4 0.7 copy-start

commit v2 on v1

v2 whole, which is shorter than its diff:
```python
import math

import jax
import jax.numpy as jnp
from jax import lax
from jax.experimental import pallas as pl
from jax.experimental.pallas import tpu as pltpu
from jax.sharding import PartitionSpec as P


QPER = 5
HD = 128
PAGE = 4
CHUNKS = PAGE + 1
NEG = -1e30
WIDE = 5
F32 = jnp.float32
BF16 = jnp.bfloat16

NT = (((1,), (1,)), ((), ()))
NN = (((1,), (0,)), ((), ()))
TN = (((0,), (0,)), ((), ()))


def dot(a, b, dims=NN):
    return lax.dot_general(a, b, dims, preferred_element_type=F32)


def shifted(x, by):
    count = lax.axis_size("seq")
    pairs = [(i, i + by) for i in range(count - by)]
    return lax.ppermute(x, "seq", pairs)


def near_core(x):
    return pltpu.with_memory_space_constraint(x, pltpu.VMEM)


def pack_kernel(keys_ref, vals_ref, owner_ref, slot_ref, own_ref, out_ref):
    for c in range(2):
        own_ref[c] = keys_ref[:, c * HD : (c + 1) * HD]
        own_ref[2 + c] = vals_ref[:, c * HD : (c + 1) * HD].T
    rows = keys_ref.shape[0]
    pages = rows // PAGE
    per = CHUNKS * 2
    total = out_ref.shape[0]
    page_i = lax.broadcasted_iota(jnp.int32, (pages, rows), 0)
    tok_i = lax.broadcasted_iota(jnp.int32, (pages, rows), 1)
    spread = (tok_i // PAGE == page_i).astype(BF16)
    owner = dot(owner_ref[...].astype(BF16), spread).astype(jnp.int32)
    slot = dot(slot_ref[...].astype(BF16), spread).astype(jnp.int32)
    within = lax.broadcasted_iota(jnp.int32, (1, rows), 1) % PAGE
    keyed, tagged, onehot = [], [], []
    lane_id = lax.broadcasted_iota(jnp.int32, (HD, rows), 0)
    for c in range(2):
        base = owner[c : c + 1] * per
        keyed += [base + within * 2, base + within * 2 + 1]
        tagged.append(jnp.where(within == 0, base + PAGE * 2, -1))
        onehot.append((slot[c : c + 1] == lane_id).astype(BF16))
    parts = []
    for c in range(2):
        parts += [keys_ref[:, c * HD : (c + 1) * HD], vals_ref[:, c * HD : (c + 1) * HD]]
    step = 2 * HD
    for begin in range(0, total, step):
        row = begin + lax.broadcasted_iota(jnp.int32, (step, rows), 0)
        acc = jnp.zeros((step, HD), F32)
        for key, part in zip(keyed, parts):
            acc += dot((row == key).astype(BF16), part)
        for key, hot in zip(tagged, onehot):
            acc += dot((row == key).astype(BF16), hot, NT)
        out_ref[begin : begin + step] = acc.astype(BF16)


def pack_pages(keys, values, owner, slot, seq_count):
    return pl.pallas_call(
        pack_kernel,
        out_shape=(
            pltpu.VMEM((4, HD, keys.shape[0]), BF16),
            pltpu.VMEM((seq_count * CHUNKS * 2, HD), BF16),
        ),
        name="pack_pages",
    )(keys, values, owner, slot)


def place_kernel(got_ref, out_ref):
    total = got_ref.shape[0]
    per = CHUNKS * 2
    sources = total // per
    pages = PAGE * 2
    slots = out_ref.shape[0] // pages
    got = got_ref[...]
    row = lax.broadcasted_iota(jnp.int32, (1, total), 1)
    source, inside = row // per, row % per
    src = lax.broadcasted_iota(jnp.int32, (sources, 1), 0)
    hot = dot((row == src * per + pages).astype(BF16), got).astype(BF16)[:, :slots]
    chosen = dot(hot, (source == src).astype(BF16), TN).astype(BF16)
    dst = lax.broadcasted_iota(jnp.int32, (slots * pages, 1), 0)
    slot = lax.broadcasted_iota(jnp.int32, (1, slots), 1)
    wide = dot((dst // pages == slot).astype(BF16), chosen).astype(BF16)
    want = (dst % PAGE) * 2 + dst % pages // PAGE
    step = 2 * HD
    for begin in range(0, slots * pages, step):
        here = slice(begin, begin + step)
        placed = jnp.where(want[here] == inside, wide[here], jnp.zeros((), BF16))
        out_ref[here] = dot(placed, got).astype(BF16)


def place_pages(got, slots):
    return pl.pallas_call(
        place_kernel,
        out_shape=jax.ShapeDtypeStruct((slots * PAGE * 2, HD), BF16),
        name="place_pages",
    )(near_core(got))


def attend_kernel(groups, first, final, *refs):
    refs = list(refs)
    mine_ref, lens_ref, q_ref = refs[:3]
    arrays = 1 + max(g[0] for g in groups)
    kv = refs[3 : 3 + arrays]
    rest = refs[3 + arrays :]
    if not first:
        top_in, tot_in, acc_in = rest[:3]
        rest = rest[3:]
    if final:
        (out_ref,) = rest
    else:
        top_ref, tot_ref, acc_ref = rest
    rows = q_ref.shape[1]
    head = pl.program_id(0)
    reqs = lens_ref.shape[1]
    base = mine_ref[0] * rows
    lens = jnp.broadcast_to(lens_ref[...], (reqs, reqs)).astype(F32)
    r_i = lax.broadcasted_iota(jnp.int32, (reqs, reqs), 0)
    e_i = lax.broadcasted_iota(jnp.int32, (reqs, reqs), 1)
    starts = jnp.sum(jnp.where(e_i < r_i, lens, 0.0), axis=1, keepdims=True) - base.astype(F32)
    lane = lax.broadcasted_iota(jnp.int32, (1, rows), 1)
    known = jnp.where(starts <= lane.astype(F32), starts, -3e7)
    begin = jnp.max(known, axis=0, keepdims=True).astype(jnp.int32)
    earliest = jnp.min(begin)
    factor = math.log2(math.e) / math.sqrt(HD)

    key_i = lax.broadcasted_iota(jnp.int32, (rows, rows), 0)
    qry_i = lax.broadcasted_iota(jnp.int32, (rows, rows), 1)

    def take(some):
        keys, vals, masks = [], [], []
        for source, index, distance in some:
            ref = kv[source]
            keys.append(ref[head] if index is None else ref[index, head])
            vals.append(ref[2 + head] if index is None else ref[index, 2 + head])
            inside = key_i >= begin + distance * rows
            masks.append(inside & (key_i <= qry_i) if distance == 0 else inside)
        k_all = jnp.concatenate(keys, axis=0)
        v_all = jnp.concatenate(vals, axis=1)
        allowed = jnp.concatenate(masks, axis=0)
        for begin_q in range(0, QPER, WIDE):
            heads = range(begin_q, min(begin_q + WIDE, QPER))
            lanes = slice(heads[0] * rows, (heads[-1] + 1) * rows)
            queries = jnp.concatenate([q_ref[0, :, q * HD : (q + 1) * HD] for q in heads], axis=0)
            scores = dot(k_all, queries, NT) * factor
            scores = jnp.where(jnp.concatenate([allowed] * len(heads), axis=1), scores, NEG)
            top = jnp.max(scores, axis=0, keepdims=True)
            if first:
                weights = jnp.exp2(scores - top)
                total = jnp.sum(weights, axis=0, keepdims=True)
                acc = dot(v_all, weights.astype(BF16))
            else:
                old = top_in[0, 0, 0:1, lanes]
                top = jnp.maximum(old, top)
                shrink = jnp.exp2(old - top)
                weights = jnp.exp2(scores - top)
                total = tot_in[0, 0, 0:1, lanes] * shrink + jnp.sum(weights, axis=0, keepdims=True)
                acc = acc_in[0, 0, :, lanes] * shrink + dot(v_all, weights.astype(BF16))
            if final:
                result = acc * (1.0 / total)
                for i, q in enumerate(heads):
                    piece = result[:, i * rows : (i + 1) * rows]
                    out_ref[0, :, q * HD : (q + 1) * HD] = piece.T.astype(BF16)
            else:
                top_ref[0, 0, 0:1, lanes] = top
                tot_ref[0, 0, 0:1, lanes] = total
                acc_ref[0, 0, :, lanes] = acc

    def skip():
        for q in range(QPER):
            lanes = slice(q * rows, (q + 1) * rows)
            if final:
                result = acc_in[0, 0, :, lanes] * (1.0 / tot_in[0, 0, 0:1, lanes])
                out_ref[0, :, q * HD : (q + 1) * HD] = result.T.astype(BF16)
            else:
                top_ref[0, 0, 0:1, lanes] = top_in[0, 0, 0:1, lanes]
                tot_ref[0, 0, 0:1, lanes] = tot_in[0, 0, 0:1, lanes]
                acc_ref[0, 0, :, lanes] = acc_in[0, 0, :, lanes]

    for used in range(1 if first else 0, len(groups) + 1):
        some = groups[:used]
        needed = used < 1 or earliest < rows - some[-1][2] * rows
        further = used < len(groups) and earliest < rows - groups[used][2] * rows
        case = True
        if used and some[-1][2]:
            case = needed
        if used < len(groups):
            case = jnp.logical_and(case, jnp.logical_not(further))
        pl.when(case)(lambda some=some: take(some) if some else skip())


def attend(mine, lengths, queries, arrays, groups, state, final):
    layers, rows, width = queries.shape
    heads = width // (QPER * HD)
    first = state is None
    grid = (heads, layers)
    stat = pl.BlockSpec((1, 1, 8, QPER * rows), lambda c, l: (c, l, 0, 0))
    accs = pl.BlockSpec((1, 1, HD, QPER * rows), lambda c, l: (c, l, 0, 0))
    q_spec = pl.BlockSpec((1, rows, QPER * HD), lambda c, l: (l, 0, c))
    in_specs = [
        pl.BlockSpec(memory_space=pltpu.SMEM),
        pl.BlockSpec(lengths.shape, lambda c, l: (0, 0)),
        q_spec,
    ]
    in_specs += [pl.BlockSpec(memory_space=pltpu.VMEM) for _ in arrays]
    state_shapes = [
        jax.ShapeDtypeStruct((heads, layers, 8, QPER * rows), F32),
        jax.ShapeDtypeStruct((heads, layers, 8, QPER * rows), F32),
        jax.ShapeDtypeStruct((heads, layers, HD, QPER * rows), F32),
    ]
    operands = [mine, lengths, queries, *map(near_core, arrays)]
    if not first:
        in_specs += [stat, stat, accs]
        operands += list(state)
    if final:
        out_shape = jax.ShapeDtypeStruct(queries.shape, BF16)
        out_specs = q_spec
    else:
        out_shape, out_specs = state_shapes, [stat, stat, accs]

    def kernel(*refs):
        attend_kernel(groups, first, final, *refs)

    return pl.pallas_call(
        kernel,
        grid=grid,
        in_specs=in_specs,
        out_specs=out_specs,
        out_shape=out_shape,
        name="attend_last" if final else "attend_part",
    )(*operands)


def shards(queries, keys, values, lengths, page_owner, page_slot):
    tok_rows = keys.shape[0]
    slots = tok_rows // PAGE * 2
    seq_count = lax.axis_size("seq")
    mine = lax.axis_index("seq").astype(jnp.int32).reshape(1)
    lens = lengths.reshape(1, -1)
    flat_q = queries.transpose(1, 0, 2)

    own, outgoing = pack_pages(keys, values, page_owner.T, page_slot.T, seq_count)
    b6 = shifted(own, 6)
    b3 = shifted(own, 3)
    b1 = shifted(own, 1)

    got = lax.all_to_all(
        outgoing.reshape(seq_count, CHUNKS, 2, HD), "seq", split_axis=0, concat_axis=0, tiled=True
    )

    b47 = shifted(jnp.stack([b3, b6]), 1)
    b2 = shifted(b1, 1)
    groups = [(0, None, 0), (1, None, 1), (2, None, 3), (3, None, 6)]
    state = attend(mine, lens, flat_q, [own, b1, b3, b6], groups, None, False)
    b58 = shifted(b47, 1)
    groups = [(0, None, 2), (1, 0, 4), (1, 1, 7)]
    state = attend(mine, lens, flat_q, [b2, b47], groups, state, False)
    out = attend(mine, lens, flat_q, [b58], [(0, 0, 5), (0, 1, 8)], state, True)
    attended = out.transpose(1, 0, 2)

    placed = place_pages(got.reshape(seq_count * CHUNKS * 2, HD), slots)
    cache_pages = (
        placed.reshape(slots, 2, PAGE, HD).transpose(0, 2, 1, 3).reshape(slots, PAGE, 2 * HD)
    )
    return (attended, cache_pages)


def solution(mesh):
    placed = (
        P(("group", "seq"), None, "head"),
        P(("group", "seq"), "head"),
        P(("group", "seq"), "head"),
        P("group"),
        P(("group", "seq"), "head"),
        P(("group", "seq"), "head"),
    )
    return jax.shard_map(
        shards,
        mesh=mesh,
        in_specs=placed,
        out_specs=(P(("group", "seq"), None, "head"), P(("group", "seq", "head"), None, None)),
        check_vma=False,
    )
```

time: 202 us -> 154 us (0.76)
  the two profiles are of different devices: /device:TPU:174 before, /device:TPU:46 now
where the time goes in v2:
time: 154 us; the launch traced here: 153 us
  starting transfers between devices  81.3 us (53%)
  waiting for transfers between devices  43.1 us (28%)
  Pallas kernels  28.2 us (18%)
    all_to_all x1, starting transfers between devices, shards(): lax.all_to_all(outgoing.reshape(seq_count, CHUNKS, 2, HD), 'seq', split_a...  52.2 us
    ppermute x6, waiting for transfers between devices, shifted(): return lax.ppermute(x, 'seq', pairs)  43.1 us
    ppermute x6, starting transfers between devices, shifted(): return lax.ppermute(x, 'seq', pairs)  29.1 us
    pallas_call x3, Pallas kernels, attend(): pl.pallas_call(kernel, grid=grid, in_specs=in_specs, out_specs=out_specs,...  23.8 us
  transfers between devices with their start and end apart: 7, of which 3 were waited for; matrix products, arithmetic and copies ran while one was open for 0% of the time, Pallas kernels for 16%

profile of v2, /device:TPU:46, one launch (start us, length us, event | category | flops | bytes accessed | tf_op | source)
XLA Modules:
  0.0 153.3 jit_solution(7359068619954796917)
XLA Ops:
  0.6 2.4 %pack_pages.1 = (bf16[4,128,128]{2,1,0:T(8,128)(2,1)S(1)}, bf16[1280,128]{1,0:T(8,128)(2,1)}) custom-call(bf16[128,256]{1,0:T(8,128)(2,1)} %keys_ref.1, bf16[128,256]{1,0:T(8,128)(2,1)} %vals_ref.1, s32[2,32]{1,0:T(2,128)} %bitcast.26, s32[2,32]{1,0:T(2,128)} %bitcast.27), custom_call_target="tpu_custom_call" | custom-call | tf_op jit(solution)/shard_map/pack_pages/pallas_call | solution.py:75
  3.0 52.2 %all-to-all-start = ((bf16[128,5,2,128]{3,2,1,0:T(2,128)(2,1)}), bf16[128,5,2,128]{3,2,1,0:T(2,128)(2,1)S(1)}, u32[]{:S(2)}, u32[]{:S(2)}) async-start(bf16[128,5,2,128]{3,2,1,0:T(2,128)(2,1)} %bitcast.8), calls=%async_computation | async-start | bytes 655360 | tf_op jit(solution)/shard_map/all_to_all | solution.py:263
  55.2 5.3 %collective-permute-start = (bf16[4,128,128]{2,1,0:T(8,128)(2,1)S(1)}, bf16[4,128,128]{2,1,0:T(8,128)(2,1)S(1)}, u32[]{:S(2)}, u32[]{:S(2)}) collective-permute-start(bf16[4,128,128]{2,1,0:T(8,128)(2,1)S(1)} %get-tuple-element.10.refs_3_), channel_id=1, source_target_pairs={{0,6},{2,8},{4,10},{6,12},{8,14},{10,16},{12,18},{14,20},{16,22},{... | collective-permute-start | bytes 393224 | tf_op jit(solution)/shard_map/ppermute | solution.py:32
  60.5 10.4 %collective-permute-start.1 = (bf16[4,128,128]{2,1,0:T(8,128)(2,1)S(1)}, bf16[4,128,128]{2,1,0:T(8,128)(2,1)S(1)}, u32[]{:S(2)}, u32[]{:S(2)}) collective-permute-start(bf16[4,128,128]{2,1,0:T(8,128)(2,1)S(1)} %get-tuple-element.10.refs_3_), channel_id=1, source_target_pairs={{0,12},{2,14},{4,16},{6,18},{8,20},{10,22},{12,24},{14,26},{16,28}... | collective-permute-start | bytes 393224 | tf_op jit(solution)/shard_map/ppermute | solution.py:32
  70.9 25.2 %collective-permute-done.refs_5_ = bf16[4,128,128]{2,1,0:T(8,128)(2,1)S(1)} collective-permute-done((bf16[4,128,128]{2,1,0:T(8,128)(2,1)S(1)}, bf16[4,128,128]{2,1,0:T(8,128)(2,1)S(1)}, u32[]{:S(2)}, u32[]{:S(2)}) %collective-permute-start) | collective-permute-done | bytes 131104 | tf_op jit(solution)/shard_map/ppermute | solution.py:32
  96.1 14.0 %collective-permute-done.1.refs_6_ = bf16[4,128,128]{2,1,0:T(8,128)(2,1)S(1)} collective-permute-done((bf16[4,128,128]{2,1,0:T(8,128)(2,1)S(1)}, bf16[4,128,128]{2,1,0:T(8,128)(2,1)S(1)}, u32[]{:S(2)}, u32[]{:S(2)}) %collective-permute-start.1) | collective-permute-done | bytes 131104 | tf_op jit(solution)/shard_map/ppermute | solution.py:32
  110.1 4.3 %collective-permute-start.2 = (bf16[2,4,128,128]{3,2,1,0:T(8,128)(2,1)S(1)}, bf16[2,4,128,128]{3,2,1,0:T(8,128)(2,1)S(1)}, u32[]{:S(2)}, u32[]{:S(2)}) collective-permute-start(bf16[2,4,128,128]{3,2,1,0:T(8,128)(2,1)S(1)} %pad_maximum_fusion), channel_id=1, source_target_pairs={{0,2},{2,4},{4,6},{6,8},{8,10},{10,12},{12,14},{14,16},{16,18},{18... | collective-permute-start | bytes 786440 | tf_op jit(solution)/shard_map/ppermute | solution.py:32
  114.5 2.6 %collective-permute-start.4 = (bf16[4,128,128]{2,1,0:T(8,128)(2,1)S(1)}, bf16[4,128,128]{2,1,0:T(8,128)(2,1)S(1)}, u32[]{:S(2)}, u32[]{:S(2)}) collective-permute-start(bf16[4,128,128]{2,1,0:T(8,128)(2,1)S(1)} %get-tuple-element.10.refs_3_), channel_id=1, source_target_pairs={{0,2},{2,4},{4,6},{6,8},{8,10},{10,12},{12,14},{14,16},{16,18},{18... | collective-permute-start | bytes 393224 | tf_op jit(solution)/shard_map/ppermute | solution.py:32
  117.1 3.9 %collective-permute-done.2.refs_4_ = bf16[2,4,128,128]{3,2,1,0:T(8,128)(2,1)S(1)} collective-permute-done((bf16[2,4,128,128]{3,2,1,0:T(8,128)(2,1)S(1)}, bf16[2,4,128,128]{3,2,1,0:T(8,128)(2,1)S(1)}, u32[]{:S(2)}, u32[]{:S(2)}) %collective-permute-start.2) | collective-permute-done | bytes 262176 | tf_op jit(solution)/shard_map/ppermute | solution.py:32
  121.0 4.2 %collective-permute-start.3 = (bf16[2,4,128,128]{3,2,1,0:T(8,128)(2,1)S(1)}, bf16[2,4,128,128]{3,2,1,0:T(8,128)(2,1)S(1)}, u32[]{:S(2)}, u32[]{:S(2)}) collective-permute-start(bf16[2,4,128,128]{3,2,1,0:T(8,128)(2,1)S(1)} %collective-permute-done.2.refs_4_), channel_id=1, source_target_pairs={{0,2},{2,4},{4,6},{6,8},{8,10},{10,12},{12,14},{14,16},{16,18},{18... | collective-permute-start | bytes 786440 | tf_op jit(solution)/shard_map/ppermute | solution.py:32
  125.2 0.0 collective-permute-done.4.refs_4_
  125.2 2.2 %collective-permute-start.5 = (bf16[4,128,128]{2,1,0:T(8,128)(2,1)S(1)}, bf16[4,128,128]{2,1,0:T(8,128)(2,1)S(1)}, u32[]{:S(2)}, u32[]{:S(2)}) collective-permute-start(bf16[4,128,128]{2,1,0:T(8,128)(2,1)S(1)} %collective-permute-done.4.refs_4_), channel_id=1, source_target_pairs={{0,2},{2,4},{4,6},{6,8},{8,10},{10,12},{12,14},{14,16},{16,18},{18... | collective-permute-start | bytes 393224 | tf_op jit(solution)/shard_map/ppermute | solution.py:32
  127.4 8.2 %attend_part.2 = (f32[2,3,8,640]{3,2,1,0:T(8,128)}, f32[2,3,8,640]{3,2,1,0:T(8,128)}, f32[2,3,128,640]{3,2,1,0:T(8,128)}) custom-call(s32[1]{0:T(128)} %bitcast.refs_0_, s32[1,64]{1,0:T(1,128)} %bitcast.23, bf16[3,128,1280]{2,1,0:T(8,128)(2,1)} %bitcast.18, bf16[4,128,128]{2,1,0:T(8,128)(2,1)S(1)} %get-tuple-element.10.refs_3_, ...), custom_call_target="tpu_custom_call" | custom-call | tf_op jit(solution)/shard_map/attend_part/pallas_call | solution.py:240
  135.7 0.0 collective-permute-done.5.refs_3_
  135.7 8.0 %attend_part.3 = (f32[2,3,8,640]{3,2,1,0:T(8,128)}, f32[2,3,8,640]{3,2,1,0:T(8,128)}, f32[2,3,128,640]{3,2,1,0:T(8,128)}) custom-call(s32[1]{0:T(128)} %bitcast.refs_0_, s32[1,64]{1,0:T(1,128)} %bitcast.24, bf16[3,128,1280]{2,1,0:T(8,128)(2,1)} %bitcast.19, bf16[4,128,128]{2,1,0:T(8,128)(2,1)S(1)} %collective-permute-done.5.refs_3_, ...), custom_call_target="tpu_custom_call" | custom-call | tf_op jit(solution)/shard_map/attend_part/pallas_call | solution.py:240
  143.7 0.0 collective-permute-done.3.refs_3_
  143.7 7.6 %attend_last.1 = bf16[3,128,1280]{2,1,0:T(8,128)(2,1)} custom-call(s32[1]{0:T(128)} %bitcast.refs_0_, s32[1,64]{1,0:T(1,128)} %bitcast.25, bf16[3,128,1280]{2,1,0:T(8,128)(2,1)} %bitcast.20, bf16[2,4,128,128]{3,2,1,0:T(8,128)(2,1)S(1)} %collective-permute-done.3.refs_3_, f32[2,3,8,640]{3,2,1,0:T(8,128)} %get-tuple-element.14.refs_4_, ...), custom_call_target="tpu_custom_call" | custom-call | tf_op jit(solution)/shard_map/attend_last/pallas_call | solution.py:240
  151.3 0.0 all-to-all-done
  151.3 2.0 %place_pages.1 = bf16[512,128]{1,0:T(8,128)(2,1)} custom-call(bf16[1280,128]{1,0:T(8,128)(2,1)S(1)} %bitcast.15), custom_call_target="tpu_custom_call" | custom-call | tf_op jit(solution)/shard_map/place_pages/pallas_call | solution.py:109
  (1 shorter events, 0.0 us)
Async XLA Ops:
  3.0 148.3 %all-to-all-start = ((bf16[128,5,2,128]{3,2,1,0:T(2,128)(2,1)}), bf16[128,5,2,128]{3,2,1,0:T(2,128)(2,1)S(1)}, u32[]{:S(2)}, u32[]{:S(2)}) async-start(bf16[128,5,2,128]{3,2,1,0:T(2,128)(2,1)} %bitcast.8), calls=%async_computation | async-start | bytes 655360 | tf_op jit(solution)/shard_map/all_to_all | solution.py:263
  55.2 40.9 %collective-permute-start = (bf16[4,128,128]{2,1,0:T(8,128)(2,1)S(1)}, bf16[4,128,128]{2,1,0:T(8,128)(2,1)S(1)}, u32[]{:S(2)}, u32[]{:S(2)}) collective-permute-start(bf16[4,128,128]{2,1,0:T(8,128)(2,1)S(1)} %get-tuple-element.10.refs_3_), channel_id=1, source_target_pairs={{0,6},{2,8},{4,10},{6,12},{8,14},{10,16},{12,18},{14,20},{16,22},{... | collective-permute-start | bytes 393224 | tf_op jit(solution)/shard_map/ppermute | solution.py:32
  60.5 49.6 %collective-permute-start.1 = (bf16[4,128,128]{2,1,0:T(8,128)(2,1)S(1)}, bf16[4,128,128]{2,1,0:T(8,128)(2,1)S(1)}, u32[]{:S(2)}, u32[]{:S(2)}) collective-permute-start(bf16[4,128,128]{2,1,0:T(8,128)(2,1)S(1)} %get-tuple-element.10.refs_3_), channel_id=1, source_target_pairs={{0,12},{2,14},{4,16},{6,18},{8,20},{10,22},{12,24},{14,26},{16,28}... | collective-permute-start | bytes 393224 | tf_op jit(solution)/shard_map/ppermute | solution.py:32
  110.1 10.9 %collective-permute-start.2 = (bf16[2,4,128,128]{3,2,1,0:T(8,128)(2,1)S(1)}, bf16[2,4,128,128]{3,2,1,0:T(8,128)(2,1)S(1)}, u32[]{:S(2)}, u32[]{:S(2)}) collective-permute-start(bf16[2,4,128,128]{3,2,1,0:T(8,128)(2,1)S(1)} %pad_maximum_fusion), channel_id=1, source_target_pairs={{0,2},{2,4},{4,6},{6,8},{8,10},{10,12},{12,14},{14,16},{16,18},{18... | collective-permute-start | bytes 786440 | tf_op jit(solution)/shard_map/ppermute | solution.py:32
  114.5 10.7 %collective-permute-start.4 = (bf16[4,128,128]{2,1,0:T(8,128)(2,1)S(1)}, bf16[4,128,128]{2,1,0:T(8,128)(2,1)S(1)}, u32[]{:S(2)}, u32[]{:S(2)}) collective-permute-start(bf16[4,128,128]{2,1,0:T(8,128)(2,1)S(1)} %get-tuple-element.10.refs_3_), channel_id=1, source_target_pairs={{0,2},{2,4},{4,6},{6,8},{8,10},{10,12},{12,14},{14,16},{16,18},{18... | collective-permute-start | bytes 393224 | tf_op jit(solution)/shard_map/ppermute | solution.py:32
  121.0 22.7 %collective-permute-start.3 = (bf16[2,4,128,128]{3,2,1,0:T(8,128)(2,1)S(1)}, bf16[2,4,128,128]{3,2,1,0:T(8,128)(2,1)S(1)}, u32[]{:S(2)}, u32[]{:S(2)}) collective-permute-start(bf16[2,4,128,128]{3,2,1,0:T(8,128)(2,1)S(1)} %collective-permute-done.2.refs_4_), channel_id=1, source_target_pairs={{0,2},{2,4},{4,6},{6,8},{8,10},{10,12},{12,14},{14,16},{16,18},{18... | collective-permute-start | bytes 786440 | tf_op jit(solution)/shard_map/ppermute | solution.py:32
  125.2 10.5 %collective-permute-start.5 = (bf16[4,128,128]{2,1,0:T(8,128)(2,1)S(1)}, bf16[4,128,128]{2,1,0:T(8,128)(2,1)S(1)}, u32[]{:S(2)}, u32[]{:S(2)}) collective-permute-start(bf16[4,128,128]{2,1,0:T(8,128)(2,1)S(1)} %collective-permute-done.4.refs_4_), channel_id=1, source_target_pairs={{0,2},{2,4},{4,6},{6,8},{8,10},{10,12},{12,14},{14,16},{16,18},{18... | collective-permute-start | bytes 393224 | tf_op jit(solution)/shard_map/ppermute | solution.py:32
